TPU v7x, 32 devices: a 4x4x1 block of a 4x4x8 slice. The times are simulated.
32 devices in a mesh: rep: 2 (over z, core), dp: 16 (over x, y).
Axes of the slice: x: 4, y: 4, z: 1, core: 2. Of those that a mesh axis runs over, the one named last changes fastest.
The devices are a block of a 4x4x8 slice.
Arguments:
- x: bfloat16 [32, 4096, 896], P(('rep', 'dp')), parts along dimension 0
- dy: bfloat16 [32, 4096, 896], P(('rep', 'dp')), parts along dimension 0
- w_gate: bfloat16 [2, 896, 2560], P(None, 'dp')
- w_up: bfloat16 [2, 896, 2560], P(None, 'dp')
- w_down: bfloat16 [2, 2560, 896], P(None, 'dp')
Outputs:
- output 1: bfloat16 [32, 4096, 896], P(('rep', 'dp')), parts along dimension 0
- output 2: bfloat16 [4, 896, 2560], P('rep', 'dp'), parts along dimension 0
- output 3: bfloat16 [4, 896, 2560], P('rep', 'dp'), parts along dimension 0
- output 4: bfloat16 [4, 2560, 896], P('rep', 'dp'), parts along dimension 0
There are 2 independent parts. A program takes and returns all parts, laid end to end along the dimension named above; an argument that names none is the same for every part.
All inputs are finite; a program needn't handle non-finite values.
Results may differ from a plain program's by a relative error of at most 0.018.
Values are sent between devices in bfloat16 or wider.
A program may use at most 768 MiB of HBM per device.

v0:
```python
import jax
import jax.numpy as jnp
from jax import lax

NAMES = ("w_gate", "w_up", "w_down")


def matmul(a, w):
    return jnp.dot(a, w, preferred_element_type=jnp.float32).astype(jnp.bfloat16)


def normed(h):
    wide = h.astype(jnp.float32)
    scale = lax.rsqrt(jnp.mean(wide**2, -1, keepdims=True) + 1e-6)
    return (wide * scale).astype(jnp.bfloat16)


def layer(h, w):
    a = normed(h)
    gate = jnp.dot(a, w["w_gate"], preferred_element_type=jnp.float32)
    up = jnp.dot(a, w["w_up"], preferred_element_type=jnp.float32)
    return h + matmul((jax.nn.silu(gate) * up).astype(jnp.bfloat16), w["w_down"])


def stack(weights, h):
    for number in range(weights["w_gate"].shape[0]):
        h = layer(h, {name: w[number] for name, w in weights.items()})
    return h


def solution(mesh):
    groups = mesh.shape["rep"]

    def step(x, dy, *weights):
        shape = x.shape
        x, dy = (t.reshape(groups, -1, *t.shape[1:]) for t in (x, dy))

        def of_a_group(x, dy):
            _, back = jax.vjp(stack, dict(zip(NAMES, weights, strict=True)), x)
            by_weights, by_x = back(dy)
            return (by_x, *(by_weights[name] for name in NAMES))

        by_x, *by_weights = jax.vmap(of_a_group)(x, dy)
        return (by_x.reshape(shape), *(t.reshape(-1, *t.shape[2:]) for t in by_weights))

    return step
```

profile of v0, /device:TPU:98, one launch (start us, length us, event | category | flops | bytes accessed | tf_op | source)
XLA Modules:
  0.0 999.2 jit_solution(17245077456268817885)
XLA Ops:
  7.2 1.9 fusion.111
  9.2 0.1 all-gather.32.cloned.1.call-start
  9.3 1.9 fusion.110
  11.2 0.1 all-gather.34.cloned.1.call-start
  11.3 1.9 fusion.109
  13.3 0.1 all-gather.36.cloned.1.call-start
  13.4 0.6 all-gather.36.cloned.1.call-update
  13.9 0.1 all-gather.40.cloned.1.call-start
  14.0 0.6 all-gather.40.cloned.1.call-update
  14.7 0.6 all-gather.38.cloned.1.call-update
  15.2 0.1 reduce-scatter.29.cloned.1.call-start
  15.3 4.6 fusion.32
  19.9 10.8 %copy.1 = bf16[1,4096,896]{1,2,0:T(8,128)(2,1)} copy(bf16[1,4096,896]{2,1,0:T(8,128)(2,1)} %param.1) | data formatting | bytes 14680064 | tf_op args[0]
  30.7 0.6 multiply_add_fusion.1
  31.3 10.8 %copy = bf16[1,4096,896]{1,2,0:T(8,128)(2,1)} copy(bf16[1,4096,896]{2,1,0:T(8,128)(2,1)} %param) | data formatting | bytes 14680064 | tf_op args[1]
  42.0 18.8 %all-gather.30.cloned.1.call-done = bf16[1,896,2560]{2,1,0:T(8,128)(2,1)} async-done(((bf16[1,56,2560]{2,1,0:T(8,128)(2,1)}), bf16[1,896,2560]{2,1,0:T(8,128)(2,1)}) %all-gather.30.cloned.1.call-update) | async-done | bytes 4587536 | tf_op jit(solution)/vmap(jvp())/squeeze | solution.py:27
  60.8 29.3 %fusion.99 = f32[4096,2560]{1,0:T(8,128)} fusion(bf16[1,896,2560]{2,1,0:T(8,128)(2,1)} %all-gather.30.cloned.1.call-done, bf16[1,4096,896]{2,1,0:T(8,128)(2,1)} %param.1, f32[4096]{0:T(1024)S(1)} %get-tuple-element.13), kind=kOutput, calls=%fused_computation.101 | convolution fusion | flops 18801491968 | bytes 53886976 | tf_op jit(solution)/vmap(jvp())/dot_general | solution.py:20
  90.1 20.7 %all-gather.32.cloned.1.call-done = bf16[1,896,2560]{2,1,0:T(8,128)(2,1)} async-done(((bf16[1,56,2560]{2,1,0:T(8,128)(2,1)}), bf16[1,896,2560]{2,1,0:T(8,128)(2,1)}) %all-gather.32.cloned.1.call-update) | async-done | bytes 4587536 | tf_op jit(solution)/vmap(jvp())/squeeze | solution.py:27
  110.9 29.4 %fusion.95 = f32[4096,2560]{1,0:T(8,128)} fusion(bf16[1,896,2560]{2,1,0:T(8,128)(2,1)} %all-gather.32.cloned.1.call-done, bf16[1,4096,896]{2,1,0:T(8,128)(2,1)} %param.1, f32[4096]{0:T(1024)S(1)} %get-tuple-element.13), kind=kOutput, calls=%fused_computation.97 | convolution fusion | flops 18801491968 | bytes 53886976 | tf_op jit(solution)/vmap(jvp())/dot_general | solution.py:21
  140.3 34.3 %fusion.24 = bf16[4096,2560]{1,0:T(8,128)(2,1)} fusion(f32[4096,2560]{1,0:T(8,128)} %fusion.95, f32[4096,2560]{1,0:T(8,128)} %fusion.99), kind=kLoop, calls=%fused_computation.43 | loop fusion | flops 62914560 | bytes 104857600
  174.6 27.3 %fusion.40 = (f32[4096]{0:T(1024)S(1)}, bf16[1,1,4096,896]{2,3,1,0:T(8,128)(2,1)}) fusion(bf16[4096,2560]{1,0:T(8,128)(2,1)} %fusion.24, bf16[1,2560,896]{2,1,0:T(8,128)(2,1)} %all-gather.34.cloned.1.call-done, bf16[1,4096,896]{1,2,0:T(8,128)(2,1)} %copy.1), kind=kOutput, calls=%fused_computation.62 | convolution fusion | flops 18808827904 | bytes 40255488 | tf_op jit(solution)/vmap(jvp())/dot_general | solution.py:9
  201.9 0.6 copy-done.2
  202.5 7.7 all-gather.36.cloned.1.call-done
  210.2 29.5 %fusion.84 = f32[4096,2560]{1,0:T(8,128)} fusion(bf16[1,1,4096,896]{2,3,1,0:T(8,128)(2,1)} %get-tuple-element.15, f32[4096]{0:T(1024)S(1)} %bitcast.298, bf16[1,896,2560]{2,1,0:T(8,128)(2,1)} %all-gather.36.cloned.1.call-done), kind=kOutput, calls=%fused_computation.87 | convolution fusion | flops 18801491968 | bytes 53886976 | tf_op jit(solution)/vmap(jvp())/dot_general | solution.py:20
  239.7 20.4 %all-gather.40.cloned.1.call-done = bf16[1,896,2560]{2,1,0:T(8,128)(2,1)} async-done(((bf16[1,56,2560]{2,1,0:T(8,128)(2,1)}), bf16[1,896,2560]{2,1,0:T(8,128)(2,1)}) %all-gather.40.cloned.1.call-update) | async-done | bytes 4587536 | tf_op jit(solution)/vmap(jvp())/squeeze | solution.py:27
  260.1 29.6 %fusion.82 = f32[4096,2560]{1,0:T(8,128)} fusion(bf16[1,1,4096,896]{2,3,1,0:T(8,128)(2,1)} %get-tuple-element.15, f32[4096]{0:T(1024)S(1)} %bitcast.299, bf16[1,896,2560]{2,1,0:T(8,128)(2,1)} %all-gather.40.cloned.1.call-done), kind=kOutput, calls=%fused_computation.86 | convolution fusion | flops 18801491968 | bytes 53886976 | tf_op jit(solution)/vmap(jvp())/dot_general | solution.py:21
  289.7 19.7 %all-gather.38.cloned.1.call-done = bf16[1,2560,896]{2,1,0:T(8,128)(2,1)} async-done(((bf16[1,160,896]{2,1,0:T(8,128)(2,1)}), bf16[1,2560,896]{2,1,0:T(8,128)(2,1)}) %all-gather.38.cloned.1.call-update) | async-done | bytes 4587536 | tf_op jit(solution)/vmap(jvp())/squeeze | solution.py:27
  309.5 28.4 %convolution_convert_fusion.1 = bf16[4096,2560]{1,0:T(8,128)(2,1)} fusion(bf16[1,4096,896]{2,1,0:T(8,128)(2,1)} %param, bf16[1,2560,896]{2,1,0:T(8,128)(2,1)} %all-gather.38.cloned.1.call-done), kind=kOutput, calls=%fused_computation.39 | convolution fusion | flops 18800967680 | bytes 32899072 | tf_op jit(solution)/vmap(transpose(jvp()))/dot_general | solution.py:9
  337.9 33.6 %fusion.4 = bf16[4096,2560]{1,0:T(8,128)(2,1)S(1)} fusion(f32[4096,2560]{1,0:T(8,128)} %fusion.84, f32[4096,2560]{1,0:T(8,128)} %fusion.82, bf16[4096,2560]{1,0:T(8,128)(2,1)} %convolution_convert_fusion.1), kind=kLoop, calls=%fused_computation.10 | loop fusion | flops 125829120 | bytes 125829120
  371.5 7.1 copy-done.1
  378.6 27.2 %fusion.89 = bf16[4096,896]{0,1:T(8,128)(2,1)} fusion(bf16[4096,2560]{1,0:T(8,128)(2,1)S(1)} %fusion.4, bf16[1,896,2560]{2,1,0:T(8,128)(2,1)} %all-gather.36.cloned.1.call-done), kind=kOutput, calls=%fused_computation.91 | convolution fusion | flops 18790481920 | bytes 32899072 | tf_op jit(solution)/vmap(transpose(jvp()))/dot_general | solution.py:20
  405.8 38.1 %fusion.42 = (f32[4096]{0:T(1024)S(1)}, bf16[4096,896]{0,1:T(8,128)(2,1)}) fusion(bf16[1,1,4096,896]{2,3,1,0:T(8,128)(2,1)} %get-tuple-element.15, bf16[4096,896]{0,1:T(8,128)(2,1)} %fusion.89, bf16[1,896,2560]{2,1,0:T(8,128)(2,1)} %all-gather.40.cloned.1.call-done, bf16[4096,2560]{1,0:T(8,128)(2,1)} %convolution_convert_fusion.1, f32[4096,2560]{1,0:T(8,128)} %fusion.84), kind=kOutput, calls=%fused_computation.64 | convolution fusion | flops 18875412480 | bytes 89538560 | tf_op jit(solution)/vmap(transpose(jvp()))/dot_general | solution.py:21
  444.0 10.3 %fusion.47 = bf16[1,1,4096,896]{2,3,1,0:T(8,128)(2,1)S(1)} fusion(bf16[1,1,4096,896]{2,3,1,0:T(8,128)(2,1)} %get-tuple-element.15, bf16[4096,896]{0,1:T(8,128)(2,1)} %get-tuple-element.17, bf16[1,4096,896]{1,2,0:T(8,128)(2,1)} %copy, f32[4096]{0:T(1024)S(1)} %bitcast.297, f32[4096]{0:T(1024)S(1)} %bitcast.300), kind=kLoop, calls=%fused_computation.69 | loop fusion | flops 25690112 | bytes 29392896 | tf_op jit(solution)/vmap(transpose(jvp()))/add_any | solution.py:13
  454.3 2.9 copy-done
  457.2 26.8 %fusion.69 = f32[1,2560,896]{2,1,0:T(8,128)} fusion(bf16[4096,2560]{1,0:T(8,128)(2,1)} %fusion.24, bf16[1,1,4096,896]{2,3,1,0:T(8,128)(2,1)S(1)} %fusion.47), kind=kOutput, calls=%fused_computation.82 | convolution fusion | flops 18790481920 | bytes 37486592 | tf_op jit(solution)/vmap(transpose(jvp()))/dot_general | solution.py:9
  484.0 0.1 reduce-scatter.27.cloned.1.call-start
  484.1 36.8 %fusion.72 = f32[1,2560,896]{2,1,0:T(8,128)} fusion(bf16[1,4096,896]{2,1,0:T(8,128)(2,1)} %param, f32[4096,2560]{1,0:T(8,128)} %fusion.82, f32[4096,2560]{1,0:T(8,128)} %fusion.84), kind=kOutput, calls=%fused_computation.84 | convolution fusion | flops 18853396480 | bytes 100401152 | tf_op jit(solution)/vmap(transpose(jvp()))/dot_general | solution.py:9
  520.9 0.1 reduce-scatter.35.cloned.1.call-start
  521.0 27.9 %convolution_convert_fusion = bf16[4096,2560]{1,0:T(8,128)(2,1)} fusion(bf16[1,1,4096,896]{2,3,1,0:T(8,128)(2,1)} %copy-done, bf16[1,2560,896]{2,1,0:T(8,128)(2,1)} %all-gather.34.cloned.1.call-done), kind=kOutput, calls=%fused_computation.38 | convolution fusion | flops 18800967680 | bytes 32899072 | tf_op jit(solution)/vmap(transpose(jvp()))/dot_general | solution.py:9
  548.9 41.2 %fusion.7 = bf16[4096,2560]{1,0:T(8,128)(2,1)} fusion(f32[4096,2560]{1,0:T(8,128)} %fusion.99, f32[4096,2560]{1,0:T(8,128)} %fusion.95, bf16[4096,2560]{1,0:T(8,128)(2,1)} %convolution_convert_fusion), kind=kLoop, calls=%fused_computation.13 | loop fusion | flops 125829120 | bytes 125829120
  590.1 34.5 %fusion.77 = f32[1,896,2560]{2,1,0:T(8,128)} fusion(bf16[4096,2560]{1,0:T(8,128)(2,1)} %convolution_convert_fusion.1, f32[4096,2560]{1,0:T(8,128)} %fusion.84, bf16[1,1,4096,896]{2,3,1,0:T(8,128)(2,1)} %get-tuple-element.15, f32[4096]{0:T(1024)S(1)} %bitcast.301), kind=kOutput, calls=%fused_computation.85 | convolution fusion | flops 18864406528 | bytes 79446016 | tf_op jit(solution)/vmap(transpose(jvp()))/dot_general | solution.py:21
  624.7 0.1 reduce-scatter.37.cloned.1.call-start
  624.8 25.1 %fusion.97 = bf16[4096,896]{0,1:T(8,128)(2,1)} fusion(bf16[4096,2560]{1,0:T(8,128)(2,1)} %fusion.7, bf16[1,896,2560]{2,1,0:T(8,128)(2,1)} %all-gather.30.cloned.1.call-done), kind=kOutput, calls=%fused_computation.99 | convolution fusion | flops 18790481920 | bytes 32899072 | tf_op jit(solution)/vmap(transpose(jvp()))/dot_general | solution.py:20
  649.9 38.1 %fusion.38 = (f32[4096]{0:T(1024)S(1)}, bf16[4096,896]{0,1:T(8,128)(2,1)}) fusion(bf16[1,4096,896]{1,2,0:T(8,128)(2,1)} %copy.1, bf16[4096,896]{0,1:T(8,128)(2,1)} %fusion.97, bf16[1,896,2560]{2,1,0:T(8,128)(2,1)} %all-gather.32.cloned.1.call-done, bf16[4096,2560]{1,0:T(8,128)(2,1)} %convolution_convert_fusion, f32[4096,2560]{1,0:T(8,128)} %fusion.99), kind=kOutput, calls=%fused_computation.60 | convolution fusion | flops 18875412480 | bytes 89538560 | tf_op jit(solution)/vmap(transpose(jvp()))/dot_general | solution.py:21
  688.0 0.7 fusion.112
  688.7 34.8 %fusion.61 = f32[1,896,2560]{2,1,0:T(8,128)} fusion(bf16[4096,2560]{1,0:T(8,128)(2,1)} %convolution_convert_fusion, f32[4096,2560]{1,0:T(8,128)} %fusion.99, bf16[1,4096,896]{1,2,0:T(8,128)(2,1)} %copy.1, f32[4096]{0:T(1024)S(1)} %bitcast.303), kind=kOutput, calls=%fused_computation.80 | convolution fusion | flops 18864406528 | bytes 79446016 | tf_op jit(solution)/vmap(transpose(jvp()))/dot_general | solution.py:21
  723.5 0.1 reduce-scatter.31.cloned.1.call-start
  723.6 25.6 %convolution_bitcast_fusion = f32[1,896,2560]{2,1,0:T(8,128)} fusion(bf16[4096,2560]{1,0:T(8,128)(2,1)} %copy-done.1, bf16[1,1,4096,896]{2,3,1,0:T(8,128)(2,1)} %get-tuple-element.15, f32[4096]{0:T(1024)S(1)} %bitcast.302), kind=kOutput, calls=%fused_computation.83 | convolution fusion | flops 18801491968 | bytes 37502976 | tf_op jit(solution)/vmap(transpose(jvp()))/dot_general | solution.py:20
  749.3 0.1 reduce-scatter.33.cloned.1.call-start
  749.3 25.6 %fusion.66 = f32[1,896,2560]{2,1,0:T(8,128)} fusion(bf16[4096,2560]{1,0:T(8,128)(2,1)} %fusion.7, bf16[1,4096,896]{1,2,0:T(8,128)(2,1)} %copy.1, f32[4096]{0:T(1024)S(1)} %bitcast.304), kind=kOutput, calls=%fused_computation.81 | convolution fusion | flops 18801491968 | bytes 37502976 | tf_op jit(solution)/vmap(transpose(jvp()))/dot_general | solution.py:20
  775.0 12.4 %fusion.46 = bf16[1,4096,896]{1,2,0:T(8,128)(2,1)} fusion(bf16[1,1,4096,896]{2,3,1,0:T(8,128)(2,1)} %copy-done, bf16[4096,896]{0,1:T(8,128)(2,1)} %get-tuple-element.19, bf16[1,4096,896]{1,2,0:T(8,128)(2,1)} %copy.1, f32[4096]{0:T(1024)S(1)} %bitcast.306, f32[4096]{0:T(1024)S(1)} %bitcast.305), kind=kLoop, calls=%fused_computation.68 | loop fusion | flops 25690112 | bytes 29392896 | tf_op jit(solution)/reshape | solution.py:44
  787.4 10.8 %copy.2 = bf16[1,4096,896]{2,1,0:T(8,128)(2,1)} copy(bf16[1,4096,896]{1,2,0:T(8,128)(2,1)} %fusion.46) | data formatting | bytes 14680064
  798.2 1.1 convert_bitcast_fusion
  799.3 1.1 convert_bitcast_fusion.1
  800.4 0.9 add_bitcast_fusion
  801.3 1.1 convert_bitcast_fusion.3
  802.4 18.2 %reduce-scatter.37.cloned.1.call-done = f32[1,56,2560]{2,1,0:T(8,128)} async-done(((f32[1,896,2560]{2,1,0:T(8,128)}), f32[1,56,2560]{2,1,0:T(8,128)}) %reduce-scatter.37.cloned.1.call-update) | async-done | bytes 573456
  820.6 1.1 convert_bitcast_fusion.2
  821.7 0.8 add_bitcast_fusion.1
  822.5 83.0 %reduce-scatter.31.cloned.1.call-done = f32[1,56,2560]{2,1,0:T(8,128)} async-done(((f32[1,896,2560]{2,1,0:T(8,128)}), f32[1,56,2560]{2,1,0:T(8,128)}) %reduce-scatter.31.cloned.1.call-update) | async-done | bytes 573456
  905.5 1.1 convert_bitcast_fusion.5
  906.5 83.6 %reduce-scatter.33.cloned.1.call-done = f32[1,56,2560]{2,1,0:T(8,128)} async-done(((f32[1,896,2560]{2,1,0:T(8,128)}), f32[1,56,2560]{2,1,0:T(8,128)}) %reduce-scatter.33.cloned.1.call-update) | async-done | bytes 573456
  990.2 1.1 convert_bitcast_fusion.4
  991.3 0.8 add_bitcast_fusion.2
  (35 shorter events, 0.7 us)
Async XLA Ops:
  7.2 53.6 %all-gather.30.cloned.1.call-start = ((), (), s32[]{:S(2)}) async-start(), calls=%async_computation.6 | async-start | bytes 4874240 | tf_op jit(solution)/vmap(jvp())/squeeze | solution.py:27
  9.2 101.6 %all-gather.32.cloned.1.call-start = ((), (), s32[]{:S(2)}) async-start(), calls=%async_computation.7 | async-start | bytes 4874240 | tf_op jit(solution)/vmap(jvp())/squeeze | solution.py:27
  11.2 163.4 %all-gather.34.cloned.1.call-start = ((), (), s32[]{:S(2)}) async-start(), calls=%async_computation.8 | async-start | bytes 4874240 | tf_op jit(solution)/vmap(jvp())/squeeze | solution.py:27
  13.3 196.9 %all-gather.36.cloned.1.call-start = ((), (), s32[]{:S(2)}) async-start(), calls=%async_computation.9 | async-start | bytes 4874240 | tf_op jit(solution)/vmap(jvp())/squeeze | solution.py:27
  13.9 246.2 %all-gather.40.cloned.1.call-start = ((), (), s32[]{:S(2)}) async-start(), calls=%async_computation.11 | async-start | bytes 4874240 | tf_op jit(solution)/vmap(jvp())/squeeze | solution.py:27
  14.6 294.9 %all-gather.38.cloned.1.call-start = ((), (), s32[]{:S(2)}) async-start(), calls=%async_computation.10 | async-start | bytes 4874240 | tf_op jit(solution)/vmap(jvp())/squeeze | solution.py:27
  15.2 783.0 %reduce-scatter.29.cloned.1.call-start = ((), (), s32[]{:S(2)}) async-start(), calls=%async_computation.13 | async-start | bytes 9748480
  201.9 0.6 copy-start.2
  202.5 57.6 %copy-start.4 = (f32[1,1,4096]{2,1,0:T(1,128)}, f32[1,1,4096]{2,1,0:T(1,128)S(1)}, u32[]{:S(2)}) copy-start(f32[1,1,4096]{2,1,0:T(1,128)S(1)} %rsqrt.23) | copy-start | bytes 49156
  371.5 7.1 copy-start.1
  405.8 38.1 %copy-start.3 = (f32[4096]{0:T(1024)S(1)}, f32[4096]{0:T(1024)}, u32[]{:S(2)}) copy-start(f32[4096]{0:T(1024)} %copy-done.2) | copy-start | bytes 49156
  405.8 38.2 %copy-start.5 = (f32[1,1,4096]{2,1,0:T(1,128)S(1)}, f32[1,1,4096]{2,1,0:T(1,128)}, u32[]{:S(2)}) copy-start(f32[1,1,4096]{2,1,0:T(1,128)} %copy-done.4) | copy-start | bytes 49156
  454.3 2.9 copy-start
  484.0 315.3 %reduce-scatter.27.cloned.1.call-start = ((), (), s32[]{:S(2)}) async-start(), calls=%async_computation.12 | async-start | bytes 9748480
  520.9 280.4 %reduce-scatter.35.cloned.1.call-start = ((), (), s32[]{:S(2)}) async-start(), calls=%async_computation.16 | async-start | bytes 9748480
  548.9 41.2 %copy-start.6 = (f32[1,1,4096]{2,1,0:T(1,128)S(1)}, f32[1,1,4096]{2,1,0:T(1,128)}, u32[]{:S(2)}) copy-start(f32[1,1,4096]{2,1,0:T(1,128)} %copy-done.4) | copy-start | bytes 49156
  624.7 195.9 %reduce-scatter.37.cloned.1.call-start = ((), (), s32[]{:S(2)}) async-start(), calls=%async_computation.17 | async-start | bytes 9748480
  649.9 38.1 %copy-start.9 = (f32[4096]{0:T(1024)S(1)}, f32[4096]{0:T(1024)}, u32[]{:S(2)}) copy-start(f32[4096]{0:T(1024)} %get-tuple-element.12) | copy-start | bytes 49156
  688.7 34.9 %copy-start.7 = (f32[1,1,4096]{2,1,0:T(1,128)S(1)}, f32[1,1,4096]{2,1,0:T(1,128)}, u32[]{:S(2)}) copy-start(f32[1,1,4096]{2,1,0:T(1,128)} %copy-done.4) | copy-start | bytes 49156
  723.5 182.0 %reduce-scatter.31.cloned.1.call-start = ((), (), s32[]{:S(2)}) async-start(), calls=%async_computation.14 | async-start | bytes 9748480
  749.2 25.8 %copy-start.8 = (f32[1,1,4096]{2,1,0:T(1,128)S(1)}, f32[1,1,4096]{2,1,0:T(1,128)}, u32[]{:S(2)}) copy-start(f32[1,1,4096]{2,1,0:T(1,128)} %get-tuple-element.11) | copy-start | bytes 49156
  749.3 240.9 %reduce-scatter.33.cloned.1.call-start = ((), (), s32[]{:S(2)}) async-start(), calls=%async_computation.15 | async-start | bytes 9748480
Sparse Core Ops, SparseCore 0:
  10.0 50.7 all-gather.29
  63.4 47.4 all-gather.31
  112.9 47.4 all-gather.33
  162.8 47.4 all-gather.35
  212.7 47.4 all-gather.39
  262.0 47.4 all-gather.37
  484.1 81.7 reduce-scatter.28
  569.2 81.6 reduce-scatter.26
  654.2 81.6 reduce-scatter.34
  739.1 81.4 reduce-scatter.36
  823.9 81.5 reduce-scatter.30
  908.6 81.5 reduce-scatter.32
where the time goes:
time: 1010 us; the launch traced here: 999 us
  matrix products  514 us (51%)
  waiting for transfers between devices  274 us (27%)
  other arithmetic  147 us (15%)
  local copies, waits for them, and re-layouts  48.7 us (5%)
  between operations  14.6 us (1%)
    dot_general x6, matrix products, layer(): up = jnp.dot(a, w['w_up'], preferred_element_type=jnp.float32)  205 us
    unnamed x18, waiting for transfers between devices  187 us
    dot_general x6, matrix products, layer(): gate = jnp.dot(a, w['w_gate'], preferred_element_type=jnp.float32)  162 us
    dot_general x5, matrix products, matmul(): jnp.dot(a, w, preferred_element_type=jnp.float32).astype(jnp.bfloat16)  147 us
    unnamed x3, other arithmetic  109 us
    squeeze x6, waiting for transfers between devices, stack(): h = layer(h, {name: w[number] for name, w in weights.items()})  87.3 us
    unnamed x23, local copies, waits for them, and re-layouts  42.9 us
  transfers between devices with their start and end apart: 12, of which 8 were waited for; matrix products, arithmetic and copies ran while one was open for 53% of the time, Pallas kernels for 0%

commit v1 on v0

v1 whole, which is shorter than its diff:
```python
import functools
import math

import jax
import jax.numpy as jnp
from jax import lax
from jax.experimental import pallas as pl
from jax.experimental.pallas import tpu as pltpu
from jax.sharding import PartitionSpec as P

F32, BF16 = jnp.float32, jnp.bfloat16
TILE = 512
PIECE = 512
CHUNK = 1280
VMEM = 63 * 1024 * 1024
NT = (((1,), (1,)), ((), ()))


def dot(a, b):
    return jnp.dot(a, b, preferred_element_type=F32)


def dot_nt(a, b):
    return lax.dot_general(a, b, NT, preferred_element_type=F32)


def norm_scale(wide):
    return lax.rsqrt(jnp.mean(wide**2, -1, keepdims=True) + 1e-6)


def normed(h):
    wide = h.astype(F32)
    return (wide * norm_scale(wide)).astype(BF16)


def backward_of_norm(h, by_a):
    wide = h.astype(F32)
    scale = norm_scale(wide)
    inner = jnp.mean(by_a * wide, -1, keepdims=True)
    return scale * by_a - wide * (scale**3 * inner)


def pieces(n):
    return [pl.ds(start, CHUNK) for start in range(0, n, CHUNK)]


def gated(gate, up, by_act):
    sig = jax.nn.sigmoid(gate)
    silu = gate * sig
    by_up = by_act * silu
    by_gate = by_act * up * (sig * (1.0 + gate * (1.0 - sig)))
    return (silu * up).astype(BF16), by_gate.astype(BF16), by_up.astype(BF16)


def forward_kernel(side, x_ref, wg_ref, wu_ref, wd_ref, *refs):
    shards, (gate_ref, up_ref, h_ref), outs, scratch = refs[:3], refs[3:6], refs[6:9], refs[9:]
    gather = Gather(side, 1, shards, outs, scratch)
    for number, when in enumerate((0, 1, 2, 5)):

        @pl.when(pl.program_id(0) == when)
        def _(number=number):
            gather.stage(number)

    a = normed(x_ref[...])
    total = None
    for at in pieces(wg_ref.shape[1]):
        gate, up = dot(a, wg_ref[:, at]), dot(a, wu_ref[:, at])
        gate_ref[:, at] = gate
        up_ref[:, at] = up
        act = (gate * jax.nn.sigmoid(gate) * up).astype(BF16)
        term = dot(act, wd_ref[at, :])
        total = term if total is None else total + term
    h_ref[...] = x_ref[...] + total.astype(BF16)

    @pl.when(pl.program_id(0) == pl.num_programs(0) - 1)
    def _():
        gather.stage(Gather.STAGES - 1)


def add_down(first, at, acc_ref, by_h_t, act):
    term = dot(by_h_t, act)

    @pl.when(first)
    def _():
        acc_ref[:, at] = term

    @pl.when(jnp.logical_not(first))
    def _():
        acc_ref[:, at] += term


def close_down(acc_ref, by_wd_ref):
    @pl.when(pl.program_id(0) == pl.num_programs(0) - 1)
    def _():
        for at in pieces(acc_ref.shape[1]):
            by_wd_ref[at, :] = acc_ref[:, at].T.astype(BF16)


def turn_kernel(h_ref, by_h_ref, wg_ref, wu_ref, wd_ref, by_gate_ref, by_up_ref, by_wd_ref, acc_ref):
    first = pl.program_id(0) == 0
    a, by_h = normed(h_ref[...]), by_h_ref[...]
    by_h_t = by_h.T
    for at in pieces(wg_ref.shape[1]):
        gate, up = dot(a, wg_ref[:, at]), dot(a, wu_ref[:, at])
        by_act = dot_nt(by_h, wd_ref[at, :]).astype(BF16).astype(F32)
        act, by_gate_ref[:, at], by_up_ref[:, at] = gated(gate, up, by_act)
        add_down(first, at, acc_ref, by_h_t, act)
    close_down(acc_ref, by_wd_ref)


def back_kernel(gate_ref, up_ref, by_h_ref, wd_ref, by_gate_ref, by_up_ref, by_wd_ref, acc_ref):
    first = pl.program_id(0) == 0
    by_h = by_h_ref[...]
    by_h_t = by_h.T
    for at in pieces(wd_ref.shape[0]):
        by_act = dot_nt(by_h, wd_ref[at, :]).astype(BF16).astype(F32)
        act, by_gate_ref[:, at], by_up_ref[:, at] = gated(gate_ref[:, at], up_ref[:, at], by_act)
        add_down(first, at, acc_ref, by_h_t, act)
    close_down(acc_ref, by_wd_ref)


def cut_of(rows):
    return -(-rows // 32) * 16


class Reduction:
    STAGES = 5

    @staticmethod
    def scratch(side, rows, columns):
        shapes = []
        for n in (cut_of(rows), rows - cut_of(rows)):
            shapes += [
                pltpu.VMEM((2, side // 2, n, columns), BF16),
                pltpu.VMEM((2, side // 2, n, columns), BF16),
                pltpu.VMEM((2, side // 2, n, columns), BF16),
                pltpu.VMEM((side, n, columns), BF16),
                pltpu.VMEM((2, side, n, columns), BF16),
                pltpu.VMEM((side, n, columns), F32),
                pltpu.VMEM((n, columns), BF16),
                pltpu.VMEM((2, n, columns), BF16),
                pltpu.VMEM((2, n, columns), BF16),
                pltpu.VMEM((2, n, columns), BF16),
            ]
        return [*shapes, pltpu.SemaphoreType.DMA((2, 12)), pltpu.SemaphoreType.DMA((2, 12)), pltpu.SemaphoreType.DMA((2, 3))]

    def __init__(self, side, t_ref, out_ref, scratch):
        self.side, self.t_ref, self.out_ref = side, t_ref, out_ref
        self.held = scratch[:10], scratch[10:20]
        self.send_sem, self.recv_sem, self.own_sem = scratch[20:]
        me = lax.axis_index("dp")
        self.at = me // side, me % side
        rows, columns = out_ref.shape
        cut = cut_of(rows)
        self.rows = pl.ds(0, cut), pl.ds(cut, rows - cut)
        width = -(-columns // 256) * 128
        self.columns = pl.ds(0, width), pl.ds(width, columns - width)
        self.halves = pl.ds(0, side // 2), pl.ds(side // 2, side - side // 2)

    def beside(self, axis, by):
        x, y = self.at
        side = self.side
        return ((x + by) % side) * side + y if axis == 0 else x * side + (y + by) % side

    def line(self, item, by, which):
        at = (self.at[item] + by) % self.side
        part = pl.ds(0, self.side) if which is None else self.halves[which]
        return self.t_ref.at[at, part, self.rows[item]] if item == 0 else self.t_ref.at[part, at, self.rows[item]]

    def own(self, item, number):
        _, own, _, mine, *_ = self.held[item]
        src, dst = (
            (self.line(item, 1, 0), own.at[0]),
            (self.line(item, -1 % self.side, 1), own.at[1]),
            (self.line(item, 0, None), mine),
        )[number]
        return pltpu.make_async_copy(src, dst, self.own_sem.at[item, number])

    def copy(self, item, number):
        passing, _, sums, _, near, _, far, far_in, last, last_in = self.held[item]
        first, second, back = item, 1 - item, self.side - 1
        low, high = self.halves
        left, right = self.columns
        src, dst, axis, by = (
            lambda: (self.line(item, self.side // 2, 0), passing.at[0], first, 1),
            lambda: (self.line(item, self.side // 2, 1), passing.at[1], first, back),
            lambda: (self.line(item, 1, 1), near.at[0, high], first, 1),
            lambda: (self.line(item, back, 0), near.at[1, low], first, back),
            lambda: (sums.at[0], near.at[0, low], first, 1),
            lambda: (sums.at[1], near.at[1, high], first, back),
            lambda: (far.at[:, left], far_in.at[0, :, left], second, 1),
            lambda: (far.at[:, right], far_in.at[1, :, right], second, back),
            lambda: (last.at[0, :, right], last_in.at[0, :, right], second, 1),
            lambda: (last.at[1, :, left], last_in.at[1, :, left], second, back),
            lambda: (last.at[0, :, left], last_in.at[0, :, left], second, 1),
            lambda: (last.at[1, :, right], last_in.at[1, :, right], second, back),
        )[number]()
        return pltpu.make_async_remote_copy(
            src_ref=src,
            dst_ref=dst,
            send_sem=self.send_sem.at[item, number],
            recv_sem=self.recv_sem.at[item, number],
            device_id={"dp": self.beside(axis, by)},
            device_id_type=MESH,
        )

    def start_direct(self):
        for k in (2, 3):
            for item in range(2):
                self.copy(item, k).start()

    def stage(self, number, greet=True):
        side = self.side
        if number == 0 and greet:
            barrier = pltpu.get_barrier_semaphore()
            for axis in range(2):
                for by in (1, side - 1):
                    pl.semaphore_signal(barrier, inc=1, device_id={"dp": self.beside(axis, by)}, device_id_type=MESH)
            pl.semaphore_wait(barrier, 4)
        if number == 0:
            for k in range(2):
                for item in range(2):
                    self.copy(item, k).start()
            for k in range(3):
                for item in range(2):
                    self.own(item, k).start()
        for item in range(2):
            passing, own, sums, mine, near, total, far, far_in, last, last_in = self.held[item]
            at = self.at[1 - item]
            ahead, behind, opposite = (at + 1) % side, (at + side - 1) % side, (at + side // 2) % side
            left, right = self.columns
            if number == 1:
                for way in range(2):
                    self.own(item, way).wait()
                    self.copy(item, way).wait_recv()
                    sums[way] = (passing[way].astype(F32) + own[way].astype(F32)).astype(BF16)
                    self.copy(item, 4 + way).start()
            if number == 2:
                self.own(item, 2).wait()
                for k in range(2, 6):
                    self.copy(item, k).wait_recv()
                for j in range(side):
                    total[j] = mine[j].astype(F32) + near[0, j].astype(F32) + near[1, j].astype(F32)
                far[...] = total[opposite].astype(BF16)
                last[0, :, right] = total[ahead, :, right].astype(BF16)
                last[1, :, left] = total[behind, :, left].astype(BF16)
                for k in range(6, 10):
                    self.copy(item, k).start()
            if number == 3:
                for way, place, part in ((0, ahead, left), (1, behind, right)):
                    self.copy(item, 6 + way).wait_recv()
                    last[way, :, part] = (total[place, :, part] + far_in[way, :, part].astype(F32)).astype(BF16)
                    self.copy(item, 10 + way).start()
            if number == 4:
                for k in range(8, 12):
                    self.copy(item, k).wait_recv()
                whole_sum = total[at] + last_in[0].astype(F32) + last_in[1].astype(F32)
                self.out_ref[self.rows[item], :] = whole_sum.astype(BF16)
                for k in range(12):
                    self.copy(item, k).wait_send()


def run_stages(reductions, when):
    for number in range(Reduction.STAGES - 1):

        @pl.when(pl.program_id(0) == when[number])
        def _(number=number):
            for n, reduction in enumerate(reductions):
                reduction.stage(number, greet=n == 0)
            if number == 0:
                for reduction in reductions:
                    reduction.start_direct()


def last_stage(reductions):
    @pl.when(pl.program_id(0) == pl.num_programs(0) - 1)
    def _():
        for reduction in reductions:
            reduction.stage(Reduction.STAGES - 1)


def weight_kernel(side, h_ref, by_gate_ref, by_up_ref, t_ref, gate_ref, up_ref, sum_ref, a_t_ref, *scratch):
    reductions = [Reduction(side, t_ref, sum_ref, scratch)]
    run_stages(reductions, (0, 2, 4, 6))
    half = pl.num_programs(0) // 2

    @pl.when(pl.program_id(0) == 0)
    def _():
        @pl.loop(0, h_ref.shape[0] // TILE)
        def _(i):
            at = pl.ds(pl.multiple_of(i * TILE, TILE), TILE)
            a_t_ref[:, at] = normed(h_ref[at, :]).T

    @pl.when(pl.program_id(0) < half)
    def _():
        gate_ref[...] = dot(a_t_ref[...], by_gate_ref[...]).astype(BF16)

    @pl.when(pl.program_id(0) >= half)
    def _():
        up_ref[...] = dot(a_t_ref[...], by_up_ref[...]).astype(BF16)

    last_stage(reductions)


def input_kernel(side, h_ref, by_h_ref, by_gate_ref, by_up_ref, wg_ref, wu_ref, t0_ref, t1_ref, out_ref, sum0_ref, sum1_ref, *scratch):
    count = len(scratch) // 2
    reductions = [Reduction(side, t0_ref, sum0_ref, scratch[:count]), Reduction(side, t1_ref, sum1_ref, scratch[count:])]
    run_stages(reductions, (0, 2, 6, 7))
    by_a = dot_nt(by_gate_ref[...], wg_ref[...]).astype(BF16).astype(F32)
    by_a += dot_nt(by_up_ref[...], wu_ref[...]).astype(BF16).astype(F32)
    by_a = by_a.astype(BF16).astype(F32)
    out_ref[...] = by_h_ref[...] + backward_of_norm(h_ref[...], by_a).astype(BF16)
    last_stage(reductions)


MESH = pl.DeviceIdType.MESH


class Gather:
    STAGES = 5

    @staticmethod
    def scratch(shards):
        return [
            *(pltpu.VMEM(t.shape[1:], BF16) for t in shards),
            pltpu.SemaphoreType.DMA((4, 12)),
            pltpu.SemaphoreType.DMA((4, 12)),
            pltpu.SemaphoreType.DMA((6,)),
        ]

    def __init__(self, side, layer, shards, outs, scratch):
        self.side, self.layer, self.shards, self.outs, self.held = side, layer, shards, outs, scratch[:3]
        self.send_sem, self.recv_sem, self.own_sem = scratch[3:]
        me = lax.axis_index("dp")
        self.at = me // side, me % side
        half = shards[2].shape[1] // 2
        self.items = [
            (shards[0], outs[0], 0, 0, shards[0].shape[1]),
            (shards[1], outs[1], 1, 0, shards[1].shape[1]),
            (shards[2], outs[2], 0, 0, half),
            (shards[2], outs[2], 1, half, half),
        ]

    def beside(self, axis, by):
        x, y = self.at
        side = self.side
        return ((x + by) % side) * side + y if axis == 0 else x * side + (y + by) % side

    def part(self, item, which):
        _, _, _, start, rows = self.items[item]
        cut = cut_of(rows)
        return pl.ds(start, cut) if which == 0 else pl.ds(start + cut, rows - cut)

    def slot(self, item, by, which):
        x, y = self.at
        _, out, axis, _, _ = self.items[item]
        at = ((x + by) % self.side, y) if axis == 0 else (x, (y + by) % self.side)
        return out.at[at[0], at[1], self.part(item, which)]

    def line(self, item, by, which):
        x, y = self.at
        _, out, axis, _, _ = self.items[item]
        if axis == 0:
            return out.at[:, (y + by) % self.side, self.part(item, which)]
        return out.at[(x + by) % self.side, :, self.part(item, which)]

    def copy(self, item, number):
        shard, _, first, _, _ = self.items[item]
        back = self.side - 1
        by, which = ((1, 0), (back, 1), (1, 1), (back, 0), (1, 0), (back, 1), (1, 0), (back, 1), (1, 1), (back, 0), (1, 0), (back, 1))[number]
        behind = -by % self.side
        if number < 4:
            src, dst = shard.at[self.layer, self.part(item, which)], self.slot(item, 0, which)
        elif number < 6:
            src = dst = self.slot(item, behind, which)
        elif number < 10:
            src = dst = self.line(item, 0, which)
        else:
            src = dst = self.line(item, behind, which)
        return pltpu.make_async_remote_copy(
            src_ref=src,
            dst_ref=dst,
            send_sem=self.send_sem.at[item, number],
            recv_sem=self.recv_sem.at[item, number],
            device_id={"dp": self.beside(first if number < 6 else 1 - first, by)},
            device_id_type=MESH,
        )

    def own(self, number):
        return pltpu.make_async_copy(self.shards[number].at[self.layer], self.held[number], self.own_sem.at[number])

    def placed(self, number):
        x, y = self.at
        return pltpu.make_async_copy(self.held[number], self.outs[number].at[x, y], self.own_sem.at[3 + number])

    def stage(self, number):
        items = range(len(self.items))
        if number == 0:
            barrier = pltpu.get_barrier_semaphore()
            for axis in range(2):
                for by in (1, self.side - 1):
                    pl.semaphore_signal(barrier, inc=1, device_id={"dp": self.beside(axis, by)}, device_id_type=MESH)
            pl.semaphore_wait(barrier, 4)
            for k in range(3):
                self.own(k).start()
        if number == 1:
            for k in range(3):
                self.own(k).wait()
                self.placed(k).start()
        if number == 2:
            for k in range(3):
                self.placed(k).wait()
        waits, starts = (((), range(4)), ((0, 1), (4, 5)), ((2, 3, 4, 5), range(6, 10)), ((6, 7), (10, 11)), ((8, 9, 10, 11), ()))[number]
        for pair in range(0, max(len(waits), len(starts)), 2):
            for item in items:
                for k in waits[pair : pair + 2]:
                    self.copy(item, k).wait_recv()
                if number in (1, 3):
                    for k in starts:
                        self.copy(item, k).start()
        if number in (0, 2):
            for pair in range(0, len(starts), 2):
                for item in items:
                    for k in starts[pair : pair + 2]:
                        self.copy(item, k).start()
        if number == 4:
            for item in items:
                for k in range(12):
                    self.copy(item, k).wait_send()


def gather_kernel(side, *refs):
    gather = Gather(side, 0, refs[:3], refs[3:6], refs[6:])
    for number in range(Gather.STAGES):
        gather.stage(number)


def gathered(side, shards):
    return [((side, side, *t.shape[1:]), BF16) for t in shards]


def gather_first(side, *shards):
    return pl.pallas_call(
        functools.partial(gather_kernel, side),
        name="gather",
        in_specs=[ANY] * 3,
        out_specs=[ANY] * 3,
        out_shape=[jax.ShapeDtypeStruct(s, t) for s, t in gathered(side, shards)],
        scratch_shapes=Gather.scratch(shards),
        compiler_params=pltpu.CompilerParams(collective_id=0, has_side_effects=True, vmem_limit_bytes=VMEM),
        cost_estimate=pl.CostEstimate(flops=60_000_000_000, bytes_accessed=60_000_000, transcendentals=0),
    )(*shards)


ANY = pl.BlockSpec(memory_space=pl.ANY)


def tiled(n):
    return pl.BlockSpec((TILE, n), lambda i: (i, 0))


def whole(*shape):
    return pl.BlockSpec(shape, lambda i: (0,) * len(shape), pipeline_mode=pl.Buffered(1))


def call(kernel, name, grid, in_specs, out_specs, out_shape, scratch, matmuls, sizes, collective=None):
    tokens, d, ff = sizes
    return pl.pallas_call(
        kernel,
        name=name,
        grid=(grid,),
        in_specs=in_specs,
        out_specs=out_specs,
        out_shape=[jax.ShapeDtypeStruct(s, t) for s, t in out_shape],
        scratch_shapes=scratch,
        compiler_params=pltpu.CompilerParams(
            dimension_semantics=("arbitrary",), vmem_limit_bytes=VMEM, collective_id=collective, has_side_effects=collective is not None
        ),
        cost_estimate=pl.CostEstimate(flops=matmuls * 2 * tokens * d * ff, bytes_accessed=matmuls * 20_000_000, transcendentals=0),
    )


def solution(mesh):
    def step(x, dy, w_gate, w_up, w_down):
        shape, x, dy = x.shape, x[0], dy[0]
        tokens, d = x.shape
        ff = w_gate.shape[2]
        sizes, steps = (tokens, d, ff), tokens // TILE
        devices = mesh.shape["dp"]
        side = math.isqrt(devices)
        shards = w_gate, w_up, w_down
        first = [t.reshape(-1, t.shape[-1]) for t in gather_first(side, *shards)]

        weights = [whole(d, ff), whole(d, ff), whole(ff, d)]
        hidden, states = ((tokens, ff), BF16), ((tokens, d), BF16)
        gate, up, h, *second = call(
            functools.partial(forward_kernel, side), "fwd", steps,
            [tiled(d), *weights, ANY, ANY, ANY], [tiled(ff), tiled(ff), tiled(d), ANY, ANY, ANY],
            [((tokens, ff), F32), ((tokens, ff), F32), states, *gathered(side, shards)], Gather.scratch(shards), 3, sizes, 7,
        )(x, *first, *shards)
        second = [t.reshape(-1, t.shape[-1]) for t in second]
        wg, wu, wd = zip(first, second, strict=True)

        backward_out = dict(
            out_specs=[tiled(ff), tiled(ff), whole(ff, d)],
            out_shape=[hidden, hidden, ((ff, d), BF16)],
            scratch=[pltpu.VMEM((d, ff), F32)],
            sizes=sizes,
        )

        def reducing(t):
            rows, columns = t.shape[0] // devices, t.shape[1]
            return (
                t.reshape(side, side, rows, columns),
                whole(rows, columns),
                ((rows, columns), BF16),
                Reduction.scratch(side, rows, columns),
            )

        def by_weight(h, by_gate, by_up, t, name, collective):
            t, spec, shape, scratch = reducing(t)
            half = ff // PIECE
            early, late = (lambda i: (0, jnp.minimum(i, half - 1))), (lambda i: (0, jnp.maximum(i - half, 0)))
            return call(
                functools.partial(weight_kernel, side), name, 2 * half,
                [whole(tokens, d), pl.BlockSpec((tokens, PIECE), early), pl.BlockSpec((tokens, PIECE), late), ANY],
                [pl.BlockSpec((d, PIECE), early), pl.BlockSpec((d, PIECE), late), spec],
                [((d, ff), BF16), ((d, ff), BF16), shape], [pltpu.VMEM((d, tokens), BF16), *scratch], 2, sizes, collective,
            )(h, by_gate, by_up, t)

        def by_input(h, by_h, by_gate, by_up, n, terms, collective):
            terms, specs, shapes, scratch = zip(*map(reducing, terms), strict=True)
            return call(
                functools.partial(input_kernel, side), f"input{n}", steps,
                [tiled(d), tiled(d), tiled(ff), tiled(ff), *weights[:2], ANY, ANY],
                [tiled(d), *specs], [states, *shapes], [*scratch[0], *scratch[1]], 2, sizes, collective,
            )(h, by_h, by_gate, by_up, wg[n], wu[n], *terms)

        by_gate, by_up, by_wd = call(
            turn_kernel, "turn", steps, [tiled(d), tiled(d), *weights], matmuls=4, **backward_out
        )(h, dy, wg[1], wu[1], wd[1])
        by_wg, by_wu, down1 = by_weight(h, by_gate, by_up, by_wd, "weights1", 1)
        by_h, gate1, up1 = by_input(h, dy, by_gate, by_up, 1, (by_wg, by_wu), 2)

        by_gate, by_up, by_wd = call(
            back_kernel, "back", steps, [tiled(ff), tiled(ff), tiled(d), weights[2]], matmuls=2, **backward_out
        )(gate, up, by_h, wd[0])
        by_wg, by_wu, down0 = by_weight(x, by_gate, by_up, by_wd, "weights0", 3)
        by_x, gate0, up0 = by_input(x, by_h, by_gate, by_up, 0, (by_wg, by_wu), 4)
        return by_x.reshape(shape), jnp.stack([gate0, gate1]), jnp.stack([up0, up1]), jnp.stack([down0, down1])

    sequences, rows, gradients = P(("rep", "dp"), None, None), P(None, "dp", None), P("rep", "dp", None)
    return jax.shard_map(
        step,
        mesh=mesh,
        in_specs=(sequences, sequences, rows, rows, rows),
        out_specs=(sequences, gradients, gradients, gradients),
        check_vma=False,
    )
```

time: 1010 us -> 614 us (0.61)
  Pallas kernels: 0 us -> 595 us
  matrix products: 514 us -> 0 us
  waiting for transfers between devices: 274 us -> 0 us
  other arithmetic: 147 us -> 3.98 us
  local copies, waits for them, and re-layouts: 48.7 us -> 6.73 us
  between operations: 14.6 us -> 0.96 us
    pallas_call x0 -> x8, Pallas kernels: none -> 595 us  [the longest x2 135 us: by_input(): call(functools.partial(input_kernel, side), f'input{n}', steps, [tiled(d)...]
    dot_general x17 -> x0, matrix products: 514 us -> none  [the longest x6 205 us: layer(): up = jnp.dot(a, w['w_up'], preferred_element_type=jnp.float32)]
    unnamed x18 -> x0, waiting for transfers between devices: 187 us -> none
    unnamed x3 -> x0, other arithmetic: 109 us -> none
    squeeze x6 -> x0, waiting for transfers between devices: 87.3 us -> none  [stack(): h = layer(h, {name: w[number] for name, w in weights.items()})]
    unnamed x23 -> x7, local copies, waits for them, and re-layouts: 42.9 us -> 6.73 us
    reshape x4 -> x0, other arithmetic: 14.9 us -> none  [the longest x1 12.4 us: step(): by_x.reshape(shape)]
    add_any x1 -> x0, other arithmetic: 10.3 us -> none  [normed(): wide = h.astype(jnp.float32)]
  transfers between devices with their start and end apart: 12 -> 0, of which waited for: 8 -> 0; matrix products, arithmetic and copies ran while one was open for 53% -> 0% of each run, Pallas kernels for 0% -> 0%
where the time goes in v1:
time: 614 us; the launch traced here: 606 us
  Pallas kernels  595 us (97%)
  local copies, waits for them, and re-layouts  6.73 us (1%)
    pallas_call x2, Pallas kernels, by_input(): call(functools.partial(input_kernel, side), f'input{n}', steps, [tiled(d)...  135 us
    pallas_call x1, Pallas kernels, step(): call(turn_kernel, 'turn', steps, [tiled(d), tiled(d), *weights], matmuls=...  110 us
    pallas_call x2, Pallas kernels, by_weight(): call(functools.partial(weight_kernel, side), name, 2 * half, [whole(token...  110 us
    pallas_call x1, Pallas kernels, step(): call(functools.partial(forward_kernel, side), 'fwd', steps, [tiled(d), *w...  89 us
    pallas_call x1, Pallas kernels, gather_first(): pl.pallas_call(functools.partial(gather_kernel, side), name='gather', in_...  82.6 us
    pallas_call x1, Pallas kernels, step(): call(back_kernel, 'back', steps, [tiled(ff), tiled(ff), tiled(d), weights...  68.3 us

profile of v1, /device:TPU:98, one launch (start us, length us, event | category | flops | bytes accessed | tf_op | source)
XLA Modules:
  0.0 606.5 jit_solution(17411769748558045073)
XLA Ops:
  0.6 82.6 %gather.1 = (bf16[4,4,56,2560]{3,2,1,0:T(8,128)(2,1)}, bf16[4,4,56,2560]{3,2,1,0:T(8,128)(2,1)}, bf16[4,4,160,896]{3,2,1,0:T(8,128)(2,1)}) custom-call(bf16[2,56,2560]{2,1,0:T(8,128)(2,1)} %refs_0_.3, bf16[2,56,2560]{2,1,0:T(8,128)(2,1)} %refs_1_.3, bf16[2,160,896]{2,1,0:T(8,128)(2,1)} %refs_2_.3), custom_call_target="tpu_custom_call" | custom-call | flops 60000002048 | bytes 60000000 | tf_op jit(solution)/shard_map/gather/pallas_call | solution.py:443
  83.3 89.0 %fwd.1 = (f32[4096,2560]{1,0:T(8,128)}, f32[4096,2560]{1,0:T(8,128)}, bf16[4096,896]{1,0:T(8,128)(2,1)}, bf16[4,4,56,2560]{3,2,1,0:T(8,128)(2,1)}, bf16[4,4,56,2...) custom-call(bf16[4096,896]{1,0:T(8,128)(2,1)} %bitcast.30, bf16[896,2560]{1,0:T(8,128)(2,1)} %bitcast.33, ...), custom_call_target="tpu_custom_call" | custom-call | flops 56371445760 | bytes 60000000 | tf_op jit(solution)/shard_map/fwd/pallas_call | solution.py:496
  172.3 110.3 %turn.1 = (bf16[4096,2560]{1,0:T(8,128)(2,1)}, bf16[4096,2560]{1,0:T(8,128)(2,1)}, bf16[2560,896]{1,0:T(8,128)(2,1)}) custom-call(bf16[4096,896]{1,0:T(8,128)(2,1)} %get-tuple-element.34.h_ref, bf16[4096,896]{1,0:T(8,128)(2,1)} %bitcast.28, bf16[896,2560]{1,0:T(8,128)(2,1)} %bitcast.39, bf16[896,2560]{1,0:T(8,128)(2,1)} %bitcast.41, bf16[2560,896]{1,0:T(8,128)(2,1)} %bitcast.48), custom_call_target="tpu_custom_call" | custom-call | flops 75161927680 | bytes 80000000 | tf_op jit(solution)/shard_map/turn/pallas_call | solution.py:539
  282.6 54.5 %weights1.1 = (bf16[896,2560]{1,0:T(8,128)(2,1)}, bf16[896,2560]{1,0:T(8,128)(2,1)}, bf16[160,896]{1,0:T(8,128)(2,1)}) custom-call(bf16[4096,896]{1,0:T(8,128)(2,1)} %get-tuple-element.34.h_ref, bf16[4096,2560]{1,0:T(8,128)(2,1)} %get-tuple-element.38.by_gate_ref, bf16[4096,2560]{1,0:T(8,128)(2,1)} %get-tuple-element.39.by_up_ref, ...), custom_call_target="tpu_custom_call" | custom-call | flops 37580963840 | bytes 40000000 | tf_op jit(solution)/shard_map/weights1/pallas_call | solution.py:524
  337.1 68.2 %input1.1 = (bf16[4096,896]{1,0:T(8,128)(2,1)}, bf16[56,2560]{1,0:T(8,128)(2,1)}, bf16[56,2560]{1,0:T(8,128)(2,1)}) custom-call(bf16[4096,896]{1,0:T(8,128)(2,1)} %get-tuple-element.34.h_ref, bf16[4096,896]{1,0:T(8,128)(2,1)} %bitcast.29, bf16[4096,2560]{1,0:T(8,128)(2,1)} %get-tuple-element.38.by_gate_ref, bf16[4096,2560]{1,0:T(8,128)(2,1)} %get-tuple-element.39.by_up_ref, ...), custom_call_target="tpu_custom_call" | custom-call | flops 37580963840 | bytes 40000000 | tf_op jit(solution)/shard_map/input1/pallas_call | solution.py:533
  405.3 68.3 %back.1 = (bf16[4096,2560]{1,0:T(8,128)(2,1)}, bf16[4096,2560]{1,0:T(8,128)(2,1)}, bf16[2560,896]{1,0:T(8,128)(2,1)}) custom-call(f32[4096,2560]{1,0:T(8,128)} %get-tuple-element.44.gate_ref, f32[4096,2560]{1,0:T(8,128)} %get-tuple-element.45.up_ref, bf16[4096,896]{1,0:T(8,128)(2,1)} %get-tuple-element.43.by_h_ref, bf16[2560,896]{1,0:T(8,128)(2,1)} %bitcast.38), custom_call_target="tpu_custom_call" | custom-call | flops 37580963840 | bytes 40000000 | tf_op jit(solution)/shard_map/back/pallas_call | solution.py:545
  473.6 55.4 %weights0.1 = (bf16[896,2560]{1,0:T(8,128)(2,1)}, bf16[896,2560]{1,0:T(8,128)(2,1)}, bf16[160,896]{1,0:T(8,128)(2,1)}) custom-call(bf16[4096,896]{1,0:T(8,128)(2,1)} %bitcast.31, bf16[4096,2560]{1,0:T(8,128)(2,1)} %get-tuple-element.46.by_gate_ref, bf16[4096,2560]{1,0:T(8,128)(2,1)} %get-tuple-element.47.by_up_ref, bf16[4,4,160,896]{3,2,1,0:T(8,128)(2,1)} %bitcast.47), custom_call_target="tpu_custom_call" | custom-call | flops 37580963840 | bytes 40000000 | tf_op jit(solution)/shard_map/weights0/pallas_call | solution.py:524
  529.0 0.0 copy-start
  529.0 0.0 copy-start.1
  529.0 0.0 copy-start.2
  529.0 66.5 %input0.1 = (bf16[4096,896]{1,0:T(8,128)(2,1)}, bf16[56,2560]{1,0:T(8,128)(2,1)}, bf16[56,2560]{1,0:T(8,128)(2,1)}) custom-call(bf16[4096,896]{1,0:T(8,128)(2,1)} %bitcast.32, bf16[4096,896]{1,0:T(8,128)(2,1)} %get-tuple-element.43.by_h_ref, bf16[4096,2560]{1,0:T(8,128)(2,1)} %get-tuple-element.46.by_gate_ref, ...), custom_call_target="tpu_custom_call" | custom-call | flops 37580963840 | bytes 40000000 | tf_op jit(solution)/shard_map/input0/pallas_call | solution.py:533
  595.5 0.0 copy-done
  595.5 0.0 copy-done.1
  595.5 2.1 pad_maximum_fusion
  597.7 0.0 copy-done.2
  597.7 1.8 pad_maximum_fusion.2
  599.5 6.7 %copy.10 = bf16[1,4096,896]{2,1,0:T(8,128)(2,1)} copy(bf16[1,4096,896]{2,1,0:T(8,128)(2,1)} %bitcast.21) | data formatting | bytes 14680064
Async XLA Ops:
  529.0 66.6 %copy-start = (bf16[56,2560]{1,0:T(8,128)(2,1)S(1)}, bf16[56,2560]{1,0:T(8,128)(2,1)}, u32[]{:S(2)}) copy-start(bf16[56,2560]{1,0:T(8,128)(2,1)} %get-tuple-element.53) | copy-start | bytes 860164
  529.0 66.6 %copy-start.1 = (bf16[56,2560]{1,0:T(8,128)(2,1)S(1)}, bf16[56,2560]{1,0:T(8,128)(2,1)}, u32[]{:S(2)}) copy-start(bf16[56,2560]{1,0:T(8,128)(2,1)} %get-tuple-element.55) | copy-start | bytes 860164
  529.0 68.7 %copy-start.2 = (bf16[160,896]{1,0:T(8,128)(2,1)S(1)}, bf16[160,896]{1,0:T(8,128)(2,1)}, u32[]{:S(2)}) copy-start(bf16[160,896]{1,0:T(8,128)(2,1)} %get-tuple-element.57) | copy-start | bytes 860164
